TPU v7x, 8 devices: a whole 2x2x1 slice. The times are simulated.
8 devices in a mesh: dp: 1 (over z), ep: 8 (over y, x, core).
Axes of the slice: x: 2, y: 2, z: 1, core: 2. Of those that a mesh axis runs over, the one named last changes fastest.
Arguments:
- hidden: bfloat16 [2048, 1024], P(('dp', 'ep'))
- k_cache: bfloat16 [2048, 128, 8, 64], P(('dp', 'ep'))
- v_cache: bfloat16 [2048, 128, 8, 64], P(('dp', 'ep'))
- seq_lens: int32 [2048], P(('dp', 'ep'))
- expert_ids: int32 [2048, 8], P(('dp', 'ep'))
- ln_attn: bfloat16 [1024], replicated
- w_q: bfloat16 [1024, 1024], replicated
- w_k: bfloat16 [1024, 512], replicated
- w_v: bfloat16 [1024, 512], replicated
- q_gain: bfloat16 [64], replicated
- k_gain: bfloat16 [64], replicated
- w_o: bfloat16 [1024, 1024], replicated
- ln_moe: bfloat16 [1024], replicated
- w_router: bfloat16 [1024, 32], replicated
- w_gate: bfloat16 [32, 1024, 512], P('ep')
- w_up: bfloat16 [32, 1024, 512], P('ep')
- w_down: bfloat16 [32, 512, 1024], P('ep')
Outputs:
- output 1: bfloat16 [2048, 1024], P(('dp', 'ep'))
- output 2: bfloat16 [2048, 128, 8, 64], P(('dp', 'ep'))
- output 3: bfloat16 [2048, 128, 8, 64], P(('dp', 'ep'))
All inputs are finite; a program needn't handle non-finite values.
Results may differ from a plain program's by a relative error of at most 0.0112857.
Values are sent between devices in bfloat16 or wider.
A program may use at most 1 GiB of HBM per device.

v0:
```python
import jax
import jax.numpy as jnp
from jax import lax
from jax.sharding import PartitionSpec as P

EPS = 1e-6
ROPE_BASE = 1000000.0


def rms_scale(values, gain_vec):
    mean_sq = jnp.mean(values * values, axis=-1, keepdims=True)
    return values * lax.rsqrt(mean_sq + EPS) * gain_vec.astype(jnp.float32)


def rotate_half(values, angles):
    half_dim = values.shape[-1] // 2
    x_low = values[..., :half_dim]
    x_high = values[..., half_dim:]
    cos_val = jnp.cos(angles)
    sin_val = jnp.sin(angles)
    return jnp.concatenate([x_low * cos_val - x_high * sin_val, x_high * cos_val + x_low * sin_val], axis=-1)


def attend(hidden, k_cache, v_cache, seq_lens, ln_attn, w_q, w_k, w_v, q_gain, k_gain, w_o):
    n_seq = hidden.shape[0]
    t_max = k_cache.shape[1]
    head_dim = q_gain.shape[0]
    n_heads = w_q.shape[1] // head_dim
    n_kv = w_k.shape[1] // head_dim
    h_f32 = hidden.astype(jnp.float32)
    x_norm = rms_scale(h_f32, ln_attn).astype(jnp.bfloat16)
    q_proj = jnp.dot(x_norm, w_q, preferred_element_type=jnp.float32).reshape(n_seq, n_heads, head_dim)
    k_proj = jnp.dot(x_norm, w_k, preferred_element_type=jnp.float32).reshape(n_seq, n_kv, head_dim)
    v_new = jnp.dot(x_norm, w_v, preferred_element_type=jnp.float32).astype(jnp.bfloat16).reshape(n_seq, n_kv, head_dim)
    inv_freq = jnp.power(ROPE_BASE, -jnp.arange(0, head_dim, 2).astype(jnp.float32) / head_dim)
    angles = seq_lens.astype(jnp.float32)[:, None, None] * inv_freq[None, None, :]
    q_rot = rotate_half(rms_scale(q_proj, q_gain), angles).astype(jnp.bfloat16)
    k_new = rotate_half(rms_scale(k_proj, k_gain), angles).astype(jnp.bfloat16)
    positions = jnp.arange(t_max, dtype=jnp.int32)
    at_slot = (positions[None, :] == seq_lens[:, None])[:, :, None, None]
    k_all = jnp.where(at_slot, k_new[:, None], k_cache)
    v_all = jnp.where(at_slot, v_new[:, None], v_cache)
    q_grp = q_rot.reshape(n_seq, n_kv, n_heads // n_kv, head_dim)
    scores = jnp.einsum('skgd,stkd->skgt', q_grp, k_all, preferred_element_type=jnp.float32) * (head_dim ** -0.5)
    visible = (positions[None, :] <= seq_lens[:, None])[:, None, None, :]
    scores = jnp.where(visible, scores, -1e30)
    att_probs = jax.nn.softmax(scores, axis=-1).astype(jnp.bfloat16)
    attn_out = jnp.einsum('skgt,stkd->skgd', att_probs, v_all, preferred_element_type=jnp.float32)
    attn_out = attn_out.astype(jnp.bfloat16).reshape(n_seq, n_heads * head_dim)
    y_res = h_f32 + jnp.dot(attn_out, w_o, preferred_element_type=jnp.float32)
    return y_res, k_all, v_all


def route_tables(expert_ids, n_experts, capacity):
    expert_range = jnp.arange(n_experts, dtype=jnp.int32)
    chosen = jnp.any(expert_ids[:, :, None] == expert_range, axis=1)
    chosen_int = chosen.astype(jnp.int32)
    rank_se = jnp.cumsum(chosen_int, axis=0) - chosen_int
    cap_range = jnp.arange(capacity, dtype=jnp.int32)
    send_map = (rank_se.T[:, None, :] == cap_range[None, :, None]) & chosen.T[:, None, :]
    slot_rank = jnp.take_along_axis(rank_se, expert_ids, axis=1)
    slot_ids = expert_ids * capacity + slot_rank
    return send_map.astype(jnp.bfloat16), slot_ids


def solution(mesh):
    n_group = mesh.shape['ep']
    row_spec = P(('dp', 'ep'), None)
    cache_spec = P(('dp', 'ep'), None, None, None)
    len_spec = P(('dp', 'ep'))
    rep_vec = P(None)
    rep_mat = P(None, None)
    exp_spec = P('ep', None, None)

    def local_step(hidden, k_cache, v_cache, seq_lens, expert_ids, ln_attn, w_q, w_k, w_v, q_gain, k_gain, w_o, ln_moe, w_router, w_gate, w_up, w_down):
        y_res, k_all, v_all = attend(hidden, k_cache, v_cache, seq_lens, ln_attn, w_q, w_k, w_v, q_gain, k_gain, w_o)
        r_norm = rms_scale(y_res, ln_moe).astype(jnp.bfloat16)
        logits = jnp.dot(r_norm, w_router, preferred_element_type=jnp.float32)
        gate_vals = jax.nn.softmax(jnp.take_along_axis(logits, expert_ids, axis=1), axis=-1)
        n_seq, n_top = expert_ids.shape
        n_experts = w_router.shape[1]
        n_local = w_gate.shape[0]
        capacity = 2 * n_seq // (n_experts // n_top)
        send_map, slot_ids = route_tables(expert_ids, n_experts, capacity)
        send_rows = jnp.einsum('ecs,sd->ecd', send_map, r_norm, preferred_element_type=jnp.float32).astype(jnp.bfloat16)
        recv_rows = lax.all_to_all(send_rows, 'ep', 0, 0, tiled=True)
        recv_rows = recv_rows.reshape(n_group, n_local, capacity, -1)
        gate_pre = jnp.einsum('secd,edf->secf', recv_rows, w_gate, preferred_element_type=jnp.float32)
        up_pre = jnp.einsum('secd,edf->secf', recv_rows, w_up, preferred_element_type=jnp.float32)
        hidden_act = (jax.nn.silu(gate_pre) * up_pre).astype(jnp.bfloat16)
        out_rows = jnp.einsum('secf,efd->secd', hidden_act, w_down, preferred_element_type=jnp.float32).astype(jnp.bfloat16)
        back_rows = lax.all_to_all(out_rows.reshape(n_group * n_local, capacity, -1), 'ep', 0, 0, tiled=True)
        picked = jnp.take(back_rows.reshape(n_experts * capacity, -1), slot_ids.reshape(-1), axis=0)
        picked = picked.reshape(n_seq, n_top, -1).astype(jnp.float32)
        moe_out = jnp.sum(gate_vals[:, :, None] * picked, axis=1)
        return (y_res + moe_out).astype(jnp.bfloat16), k_all, v_all

    return jax.shard_map(local_step, mesh=mesh, in_specs=(row_spec, cache_spec, cache_spec, len_spec, row_spec, rep_vec, rep_mat, rep_mat, rep_mat, rep_vec, rep_vec, rep_mat, rep_vec, rep_mat, exp_spec, exp_spec, exp_spec), out_specs=(row_spec, cache_spec, cache_spec), check_vma=False)
```

profile of v0, /device:TPU:0, one launch (start us, length us, event | category | flops | bytes accessed | tf_op | source)
XLA Modules:
  0.0 355.8 jit_solution(16573783241577773495)
XLA Ops:
  3.6 1.2 fusion.23
  4.9 2.0 multiply_reduce_fusion.3
  7.6 1.9 convolution_convert_fusion.2
  10.0 2.0 multiply_reduce_fusion.2
  12.4 0.9 copy.66
  13.4 0.9 copy.65
  14.4 44.0 %broadcast_select_fusion.1 = (bf16[256,128,8,64]{1,3,2,0:T(8,128)(2,1)}, bf16[256,128,8,64]{1,3,2,0:T(8,128)(2,1)}) fusion(bf16[256,128,8,64]{1,3,2,0:T(8,128)(2,1)} %param.18, pred[256,128]{1,0:T(8,128)(4,1)S(1)} %get-tuple-element.15, bf16[256,8,64]{2,1,0:T(8,128)(2,1)S(1)} %copy.68, bf16[256,128,8,64]{1,3,2,0:T(8,128)(2,1)} %param.19, ...), kind=kLoop, calls=%fused_computation.5 | loop fusion | flops 33554432 | bytes 134774784 | tf_op jit(solution)/shard_map/jit(_where)/select_n | solution.py:41
  58.4 15.8 %fusion.44 = (f32[256,8,2]{2,1,0:T(8,128)S(1)}, f32[256,8,2,128]{3,2,1,0:T(2,128)}) fusion(pred[256,128]{1,0:T(8,128)(4,1)S(1)} %get-tuple-element.14, bf16[256,128,8,64]{1,3,2,0:T(8,128)(2,1)} %get-tuple-element.10, bf16[256,8,2,32]{3,2,1,0:T(2,128)(2,1)S(1)} %bitcast.95, bf16[256,8,2,32]{3,2,1,0:T(2,128)(2,1)S(1)} %bitcast.96), kind=kOutput, calls=%fused_computation.93 | convolution fusion | flops 70254720 | bytes 36225024 | tf_op jit(solution)/shard_map/sub | solution.py:47
  74.2 22.5 %convolution_convert_fusion.1 = bf16[256,8,2,64]{3,2,1,0:T(2,128)(2,1)S(1)} fusion(bf16[256,128,8,64]{1,3,2,0:T(8,128)(2,1)} %get-tuple-element.11, f32[256,8,2,128]{3,2,1,0:T(2,128)} %get-tuple-element.21, f32[256,8,2]{2,1,0:T(8,128)S(1)} %get-tuple-element.20), kind=kOutput, calls=%fused_computation.35 | convolution fusion | flops 68419584 | bytes 36192256 | tf_op jit(solution)/shard_map/skgt,stkd->skgd/dot_general | solution.py:48
  96.7 1.0 copy.71
  98.7 2.4 multiply_reduce_fusion.1
  101.1 2.5 convolution_convert_fusion
  103.6 98.1 %all_to_all.10 = bf16[32,128,1024]{2,1,0:T(8,128)(2,1)S(1)} all-to-all(bf16[32,128,1024]{2,1,0:T(8,128)(2,1)S(1)} %convolution_convert_fusion), channel_id=1, replica_groups=mesh['dp'=1,'ep'=8] {'ep'}, dimensions={0} | all-to-all | bytes 16777216 | tf_op jit(solution)/shard_map/all_to_all | solution.py:86
  201.7 3.2 copy-done.2
  204.9 6.6 %fusion.5 = f32[4,8,128,512]{3,2,1,0:T(8,128)} fusion(bf16[8,4,128,1024]{3,2,1,0:T(8,128)(2,1)S(1)} %bitcast.93, bf16[4,1024,512]{2,1,0:T(8,128)(2,1)S(1)} %copy-done.7), kind=kOutput, calls=%fused_computation.15 | convolution fusion | flops 4294967296 | bytes 20971520 | tf_op jit(solution)/shard_map/secd,edf->secf/dot_general | solution.py:89
  211.6 16.4 %convert_bitcast_fusion = bf16[8,4,128,1024]{3,2,0,1:T(8,128)(2,1)} fusion(f32[4,8,128,512]{3,2,1,0:T(8,128)} %fusion.5, bf16[8,4,128,1024]{3,2,1,0:T(8,128)(2,1)} %bitcast.94, bf16[4,512,1024]{2,1,0:T(8,128)(2,1)} %param.33, bf16[4,1024,512]{2,1,0:T(8,128)(2,1)} %param.31), kind=kOutput, calls=%fused_computation.14 | convolution fusion | flops 8606711808 | bytes 33554432 | tf_op jit(solution)/shard_map/secf,efd->secd/dot_general | solution.py:91
  228.0 8.2 %copy.81 = bf16[8,4,128,1024]{3,2,1,0:T(8,128)(2,1)} copy(bf16[8,4,128,1024]{3,2,0,1:T(8,128)(2,1)} %convert_bitcast_fusion) | data formatting | bytes 16777216 | tf_op jit(solution)/shard_map/convert_element_type | solution.py:91
  236.1 3.7 %all-to-all-start.1 = ((bf16[32,128,1024]{2,1,0:T(8,128)(2,1)}), bf16[32,128,1024]{2,1,0:T(8,128)(2,1)}, u32[]{:S(2)}, u32[]{:S(2)}) async-start(bf16[32,128,1024]{2,1,0:T(8,128)(2,1)} %bitcast.92), calls=%async_computation.1 | async-start | bytes 16777216 | tf_op jit(solution)/shard_map/all_to_all | solution.py:92
  240.2 16.8 %gather_fusion.2 = s32[2048]{0:T(1024)S(1)} fusion(s32[256,32]{0,1:T(8,128)S(1)} %fusion.32, s32[2048]{0:T(1024)S(1)} %reshape.286), kind=kCustom, calls=%fused_computation.2 | custom fusion | bytes 32768 | tf_op jit(solution)/shard_map/jit(take_along_axis)/gather | solution.py:61
  257.7 16.8 %gather_fusion.1 = f32[2048]{0:T(1024)S(1)} fusion(f32[256,32]{0,1:T(8,128)S(1)} %fusion.38, s32[2048]{0:T(1024)S(1)} %reshape.286), kind=kCustom, calls=%fused_computation.1 | custom fusion | bytes 32768 | tf_op jit(solution)/shard_map/jit(take_along_axis)/gather | solution.py:79
  275.1 58.7 %all-to-all-done.1 = bf16[32,128,1024]{2,1,0:T(8,128)(2,1)} async-done(((bf16[32,128,1024]{2,1,0:T(8,128)(2,1)}), bf16[32,128,1024]{2,1,0:T(8,128)(2,1)}, u32[]{:S(2)}, u32[]{:S(2)}) %all-to-all-start.1) | async-done | bytes 8388640 | tf_op jit(solution)/shard_map/all_to_all | solution.py:92
  333.8 15.6 %gather_fusion = bf16[2048,1024]{1,0:T(8,128)(2,1)} fusion(bf16[4096,1024]{1,0:T(8,128)(2,1)} %bitcast.21, s32[2048]{0:T(1024)S(1)} %broadcast_clamp_fusion), kind=kCustom, calls=%fused_computation | custom fusion | bytes 8396800 | tf_op jit(solution)/shard_map/jit(_take)/gather | solution.py:93
  349.4 5.4 %multiply_reduce_fusion = f32[256,1024]{1,0:T(8,128)S(1)} fusion(bf16[2048,1024]{1,0:T(8,128)(2,1)} %gather_fusion, f32[256,8]{1,0:T(8,128)S(1)} %copy.74, pred[256,8]{1,0:T(8,128)(4,1)S(1)} %copy.78), kind=kLoop, calls=%fused_computation.13 | loop fusion | flops 8126464 | bytes 5253120 | tf_op jit(solution)/shard_map/reduce_sum | solution.py:95
  354.9 0.9 add_convert_fusion
  (63 shorter events, 7.1 us)
Async XLA Ops:
  0.6 9.3 %copy-start = (bf16[1024,1024]{1,0:T(8,128)(2,1)S(1)}, bf16[1024,1024]{1,0:T(8,128)(2,1)}, u32[]{:S(2)}) copy-start(bf16[1024,1024]{1,0:T(8,128)(2,1)} %param.23) | copy-start | bytes 6291460
  0.6 9.3 %copy-start.8 = (bf16[64]{0:T(256)(128)(2,1)S(1)}, bf16[64]{0:T(256)(128)(2,1)}, u32[]{:S(2)}) copy-start(bf16[64]{0:T(256)(128)(2,1)} %param.26) | copy-start | bytes 388
  74.2 23.5 %copy-start.4 = (s32[256,8]{0,1:T(8,128)S(1)}, s32[256,8]{0,1:T(8,128)}, u32[]{:S(2)}) copy-start(s32[256,8]{0,1:T(8,128)} %param.21) | copy-start | bytes 24580
  74.2 24.5 %copy-start.6 = (bf16[1024]{0:T(1024)(128)(2,1)S(1)}, bf16[1024]{0:T(1024)(128)(2,1)}, u32[]{:S(2)}) copy-start(bf16[1024]{0:T(1024)(128)(2,1)} %param.29) | copy-start | bytes 6148
  74.2 24.5 %copy-start.3 = (bf16[256,1024]{1,0:T(8,128)(2,1)S(1)}, bf16[256,1024]{1,0:T(8,128)(2,1)}, u32[]{:S(2)}) copy-start(bf16[256,1024]{1,0:T(8,128)(2,1)} %param.17) | copy-start | bytes 1572868
  103.6 101.3 %copy-start.7 = (bf16[4,1024,512]{2,1,0:T(8,128)(2,1)S(1)}, bf16[4,1024,512]{2,1,0:T(8,128)(2,1)}, u32[]{:S(2)}) copy-start(bf16[4,1024,512]{2,1,0:T(8,128)(2,1)} %param.32) | copy-start | bytes 12582916
  201.7 3.2 copy-start.2
  236.1 97.7 %all-to-all-start.1 = ((bf16[32,128,1024]{2,1,0:T(8,128)(2,1)}), bf16[32,128,1024]{2,1,0:T(8,128)(2,1)}, u32[]{:S(2)}, u32[]{:S(2)}) async-start(bf16[32,128,1024]{2,1,0:T(8,128)(2,1)} %bitcast.92), calls=%async_computation.1 | async-start | bytes 16777216 | tf_op jit(solution)/shard_map/all_to_all | solution.py:92
  240.2 17.2 %copy-start.5 = (bf16[1024,32]{0,1:T(8,128)(2,1)S(1)}, bf16[1024,32]{0,1:T(8,128)(2,1)}, u32[]{:S(2)}) copy-start(bf16[1024,32]{0,1:T(8,128)(2,1)} %param.30) | copy-start | bytes 196612
  333.8 22.0 %copy-start.1 = (bf16[1024,1024]{1,0:T(8,128)(2,1)S(1)}, bf16[1024,1024]{1,0:T(8,128)(2,1)}, u32[]{:S(2)}) copy-start(bf16[1024,1024]{1,0:T(8,128)(2,1)} %param.23) | copy-start | bytes 6291460
where the time goes:
time: 356 us
  blocking collectives  98.1 us (28%)
  matrix products  72.4 us (20%)
  local copies, waits for them, and re-layouts  65.5 us (18%)
  waiting for transfers between devices  58.7 us (16%)
  other arithmetic  56.3 us (16%)
  starting transfers between devices  3.7 us (1%)
    all_to_all x1, blocking collectives, local_step(): recv_rows = lax.all_to_all(send_rows, 'ep', 0, 0, tiled=True)  98.1 us
    all_to_all x1, waiting for transfers between devices, local_step(): lax.all_to_all(out_rows.reshape(n_group * n_local, capacity, -1), 'ep', 0...  58.7 us
    select_n x1, other arithmetic, attend(): k_all = jnp.where(at_slot, k_new[:, None], k_cache)  44 us
    dot_general x1, matrix products, attend(): jnp.einsum('skgt,stkd->skgd', att_probs, v_all, preferred_element_type=jn...  22.5 us
    gather x5, local copies, waits for them, and re-layouts, local_step(): jnp.take_along_axis(logits, expert_ids, axis=1)  17.2 us
    gather x3, local copies, waits for them, and re-layouts, route_tables(): slot_rank = jnp.take_along_axis(rank_se, expert_ids, axis=1)  16.9 us
    dot_general x1, matrix products, local_step(): jnp.einsum('secf,efd->secd', hidden_act, w_down, preferred_element_type=j...  16.4 us
    sub x1, matrix products, attend(): att_probs = jax.nn.softmax(scores, axis=-1).astype(jnp.bfloat16)  15.8 us
  transfers between devices with their start and end apart: 1, of which 1 were waited for; matrix products, arithmetic and copies ran while one was open for 10% of the time, Pallas kernels for 0%

commit v1 on v0

v1 whole, which is shorter than its diff:
```python
import functools
import numpy as np
import jax, jax.numpy as jnp
from jax import lax
from jax.experimental import pallas as pl
from jax.experimental.pallas import tpu as pltpu
from jax.sharding import PartitionSpec as P
EPS=1e-6; ROPE_BASE=1e6
F32=jnp.float32; BF=jnp.bfloat16

def attn_body(cfg, lens_s, lens_ref, ids_ref, vec_ref, gain_ref, freq_ref, h_hbm, wq_hbm, wk_hbm, wv_hbm, wo_hbm, wr_ref, k_hbm, v_hbm,
              ko_hbm, vo_hbm, y_ref, r_ref, gt_ref,
              kb, vb, wq, wk, wv, woe, woo, h_ref, qe_ref, qo_ref, kt_ref, vt_ref, ae_ref, ao_ref, isem, osem, wsem):
    sb, nb, lag = cfg
    n = h_ref.shape[0]
    steps = n // sb
    per = 128 // sb
    n_kv, hd, dk = 8, 64, 512
    def cin(g, which):
        s = lax.rem(g, nb)
        r, b = ((k_hbm, kb), (v_hbm, vb))[which]
        return pltpu.make_async_copy(r.at[pl.ds(g*sb, sb)], b.at[s], isem.at[which, s])
    def cout(g, which):
        s = lax.rem(g, nb)
        r, b = ((ko_hbm, kb), (vo_hbm, vb))[which]
        return pltpu.make_async_copy(b.at[s], r.at[pl.ds(g*sb, sb)], osem.at[which, s])
    wcopies = [pltpu.make_async_copy(a, b, wsem.at[i]) for i, (a, b) in enumerate(
        ((h_hbm, h_ref), (wq_hbm, wq), (wk_hbm, wk), (wv_hbm, wv), (wo_hbm.at[:, 0], woe), (wo_hbm.at[:, 1], woo)))]
    for c in wcopies[:4]:
        c.start()
    for g in range(nb):
        cin(g, 0).start(); cin(g, 1).start()
    for c in wcopies[4:]:
        c.start()
    for c in wcopies[:4]:
        c.wait()
    h = h_ref[...].astype(F32)
    x = (h * lax.rsqrt(jnp.mean(h*h, axis=-1, keepdims=True) + EPS) * vec_ref[0:1, :]).astype(BF)
    ang = freq_ref[...] * lens_ref[...].astype(F32)
    cos_v = jnp.cos(ang)[None]; sin_v = jnp.sin(ang)[None]
    half = hd // 2
    def norm_rope(w_ref, gain):
        p = jnp.dot(x, w_ref[...], preferred_element_type=F32)
        p = p.T.reshape(-1, hd, n)
        p = p * lax.rsqrt(jnp.mean(p*p, axis=1, keepdims=True) + EPS) * gain[None]
        lo, hi = p[:, :half], p[:, half:]
        return jnp.concatenate([lo*cos_v - hi*sin_v, hi*cos_v + lo*sin_v], axis=1)
    q = norm_rope(wq, gain_ref[:, 0:1])
    q = q.reshape(n_kv, 2, hd, n)
    qe_ref[...] = q[:, 0].reshape(dk, n).T
    qo_ref[...] = q[:, 1].reshape(dk, n).T
    k = norm_rope(wk, gain_ref[:, 1:2]).reshape(dk, n).astype(BF).astype(F32)
    v = jnp.dot(x, wv[...], preferred_element_type=F32).T.astype(BF).astype(F32)
    for c in range(n // 128):
        kt_ref[c] = k[:, 128*c:128*c+128]
        vt_ref[c] = v[:, 128*c:128*c+128]

    lane = lax.broadcasted_iota(jnp.int32, (1, 128), 1)
    row = lax.broadcasted_iota(jnp.int32, (16, dk), 0)
    col = lax.broadcasted_iota(jnp.int32, (16, dk), 1) // hd
    m_even = row == col
    m_odd = row == col + n_kv

    @pl.loop(0, steps)
    def _(g):
        slot = lax.rem(g, nb)
        @pl.when((g >= lag) & (g - lag + nb < steps))
        def _():
            cout(g - lag, 0).wait(); cout(g - lag, 1).wait()
            cin(g - lag + nb, 0).start(); cin(g - lag + nb, 1).start()
        cin(g, 0).wait(); cin(g, 1).wait()
        base = lax.rem(g, per) * sb
        hf = g // per
        rows = pl.ds(pl.multiple_of(g*sb, sb), sb)
        qe = qe_ref[rows, :]
        qo = qo_ref[rows, :]
        hits = []; sc = []
        for p in range(sb // 2):
            ks = []; qs = []
            for i in (2*p, 2*p+1):
                ln = lens_s[g*sb + i]
                hits.append(lane == ln)
                kc = pltpu.roll(kt_ref[hf], lax.rem(ln - (base + i) + 128, 128), 1).astype(BF)
                kn = jnp.where(hits[i], kc, kb[slot, i])
                kb[slot, i] = kn
                ks.append(kn)
                qs.append(jnp.where(m_even, qe[i:i+1], jnp.where(m_odd, qo[i:i+1], 0.0)).astype(BF))
            s = jnp.dot(jnp.concatenate(qs, axis=0), jnp.concatenate(ks, axis=1), preferred_element_type=F32)
            for j in (0, 1):
                vis = lane <= lens_s[g*sb + 2*p + j]
                sc.append(jnp.where(vis, s[16*j:16*j+16, 128*j:128*j+128] * (hd ** -0.5), -1e30))
        cout(g, 0).start()
        for i in range(sb):
            ln = lens_s[g*sb + i]
            vc = pltpu.roll(vt_ref[hf], lax.rem(ln - (base + i) + 128, 128), 1).astype(BF)
            vb[slot, i] = jnp.where(hits[i], vc, vb[slot, i])
        cout(g, 1).start()
        s = jnp.concatenate(sc, axis=0)
        e = jnp.exp(s - jnp.max(s, axis=-1, keepdims=True))
        pr = (e / jnp.sum(e, axis=-1, keepdims=True)).astype(BF)
        zz = jnp.zeros((16, 128), BF)
        oe = []; oo = []
        for p in range(sb // 2):
            p0 = pr[32*p:32*p+16]; p1 = pr[32*p+16:32*p+32]
            pp = jnp.concatenate([jnp.concatenate([p0, zz], axis=1), jnp.concatenate([zz, p1], axis=1)], axis=0)
            vv = jnp.concatenate([vb[slot, 2*p], vb[slot, 2*p+1]], axis=1)
            o = lax.dot_general(pp, vv, (((1,), (1,)), ((), ())), preferred_element_type=F32)
            for j in (0, 1):
                oj = o[16*j:16*j+16]
                oe.append(jnp.sum(jnp.where(m_even[:8], oj[:8], 0.0), axis=0, keepdims=True))
                oo.append(jnp.sum(jnp.where(m_even[:8], oj[8:], 0.0), axis=0, keepdims=True))
        ae_ref[rows, :] = jnp.concatenate(oe, axis=0)
        ao_ref[rows, :] = jnp.concatenate(oo, axis=0)

    for c in wcopies[4:]:
        c.wait()
    y = h_ref[...].astype(F32)
    y = y + (jnp.dot(ae_ref[...].astype(BF), woe[...].reshape(dk, -1), preferred_element_type=F32)
             + jnp.dot(ao_ref[...].astype(BF), woo[...].reshape(dk, -1), preferred_element_type=F32))
    y_ref[...] = y
    r = (y * lax.rsqrt(jnp.mean(y*y, axis=-1, keepdims=True) + EPS) * vec_ref[1:2, :]).astype(BF)
    r_ref[...] = r
    lg = lax.dot_general(wr_ref[...], r, (((1,), (1,)), ((), ())), preferred_element_type=F32)
    eid = lax.broadcasted_iota(jnp.int32, lg.shape, 0)
    ids = ids_ref[...]
    hot = eid == ids[0:1]
    for j in range(1, ids.shape[0]):
        hot = hot | (eid == ids[j:j+1])
    lg = jnp.where(hot, lg, -jnp.inf)
    e = jnp.where(hot, jnp.exp(lg - jnp.max(lg, axis=0, keepdims=True)), 0.0)
    gt_ref[...] = e / jnp.sum(e, axis=0, keepdims=True)
    for j in range(nb):
        cout(steps - nb + j, 0).wait(); cout(steps - nb + j, 1).wait()

def attn_call(hidden, k_cache, v_cache, seq_lens, expert_ids, ln_attn, w_q, w_k, w_v, q_gain, k_gain, w_o, ln_moe, w_router, cfg=(8, 8, 3)):
    n, d = hidden.shape
    t = k_cache.shape[1]; dk = w_k.shape[1]; hd = q_gain.shape[0]; nk = dk // hd
    kc = k_cache.transpose(0, 2, 3, 1).reshape(n, dk, t)
    vc = v_cache.transpose(0, 2, 3, 1).reshape(n, dk, t)
    vec = jnp.stack([ln_attn, ln_moe]).astype(F32)
    gain = jnp.stack([q_gain, k_gain], axis=1).astype(F32)
    freq = jnp.asarray(np.power(np.float32(ROPE_BASE), -np.arange(0, hd, 2).astype(np.float32) / np.float32(hd)).astype(np.float32).reshape(-1, 1))
    sb, nb, lag = cfg
    vm = pl.BlockSpec(memory_space=pltpu.VMEM)
    an = pl.BlockSpec(memory_space=pl.ANY)
    sm = pl.BlockSpec(memory_space=pltpu.SMEM)
    ne = w_router.shape[1]
    out = pl.pallas_call(functools.partial(attn_body, cfg),
        out_shape=(jax.ShapeDtypeStruct(kc.shape, BF), jax.ShapeDtypeStruct(vc.shape, BF), jax.ShapeDtypeStruct((n, d), F32),
                   jax.ShapeDtypeStruct((n, d), BF), jax.ShapeDtypeStruct((ne, n), F32)),
        in_specs=[sm, vm, vm, vm, vm, vm, an, an, an, an, an, vm, an, an],
        out_specs=(an, an, vm, vm, vm),
        scratch_shapes=[pltpu.VMEM((nb, sb, dk, t), BF), pltpu.VMEM((nb, sb, dk, t), BF),
            pltpu.VMEM(w_q.shape, BF), pltpu.VMEM(w_k.shape, BF), pltpu.VMEM(w_v.shape, BF),
            pltpu.VMEM((nk, hd, d), BF), pltpu.VMEM((nk, hd, d), BF), pltpu.VMEM((n, d), BF),
            pltpu.VMEM((n, dk), F32), pltpu.VMEM((n, dk), F32), pltpu.VMEM((n//128, dk, 128), F32), pltpu.VMEM((n//128, dk, 128), F32),
            pltpu.VMEM((n, dk), F32), pltpu.VMEM((n, dk), F32),
            pltpu.SemaphoreType.DMA((2, nb)), pltpu.SemaphoreType.DMA((2, nb)), pltpu.SemaphoreType.DMA((6,))],
        compiler_params=pltpu.CompilerParams(vmem_limit_bytes=60<<20), name="attn",
        cost_estimate=pl.CostEstimate(flops=8*10**9, bytes_accessed=140*10**6, transcendentals=0),
    )(seq_lens, seq_lens.reshape(1, n), expert_ids.T, vec, gain, freq, hidden, w_q, w_k, w_v,
      w_o.reshape(nk, 2, hd, d), w_router.T, kc, vc)
    ko, vo, y, r, gt = out
    back = lambda z: z.reshape(n, nk, hd, t).transpose(0, 3, 1, 2)
    return back(ko), back(vo), y, r, gt


def moe_body(r_ref, gt_ref, y_ref, wg_own, wu_own, wd_own, wg_par, wu_par, wd_par, out_ref,
             wg, wu, wd, xr, gts, acc, rbuf, wsem, agsem_s, agsem_r, rssem_s, rssem_r):
    me = lax.axis_index('ep')
    core = me % 2
    xpos = (me // 2) % 2
    ypos = me // 4
    peers = [None, ypos*4 + (1-xpos)*2 + core, (1-ypos)*4 + xpos*2 + core, (1-ypos)*4 + (1-xpos)*2 + core]
    n_loc = wg_own.shape[0]
    n_exp = 2*n_loc
    half = acc.shape[-1]
    n = acc.shape[2]

    def wcopy(e, own):
        src = (wg_own, wu_own, wd_own) if own else (wg_par, wu_par, wd_par)
        s = lax.rem(e, n_loc)
        return [pltpu.make_async_copy(a.at[s], b.at[e], wsem.at[i, e]) for i, (a, b) in enumerate(zip(src, (wg, wu, wd)))]
    for e in range(n_exp):
        for c in wcopy(jnp.int32(e), e < n_loc):
            c.start()

    barrier = pltpu.get_barrier_semaphore()
    for p in peers[1:]:
        pl.semaphore_signal(barrier, inc=1, device_id={"ep": p}, device_id_type=pl.DeviceIdType.MESH)
    pl.semaphore_wait(barrier, 3)

    def remote(src, dst, ss, rs, p):
        return pltpu.make_async_remote_copy(src_ref=src, dst_ref=dst, send_sem=ss, recv_sem=rs,
                                            device_id={"ep": p}, device_id_type=pl.DeviceIdType.MESH)
    ag = {}
    for b in (3, 1, 2):
        rows8 = pl.ds(pl.multiple_of((peers[b] // 2) * n_exp, n_exp), n_exp)
        ag[b] = [remote(r_ref, xr.at[b-1], agsem_s.at[0, b-1], agsem_r.at[0, b-1], peers[b]),
                 remote(gt_ref.at[rows8], gts.at[b-1], agsem_s.at[1, b-1], agsem_r.at[1, b-1], peers[b])]
        for c in ag[b]:
            c.start()

    lane8 = lax.broadcasted_iota(jnp.int32, (n, n_exp), 1)

    def compute(b, first):
        x_view = r_ref if b == 0 else xr.at[b-1]
        if b == 0:
            g8 = gt_ref[pl.ds(pl.multiple_of((me // 2) * n_exp, n_exp), n_exp), :]
        else:
            g8 = gts[b-1]
        g8 = g8.T
        def step(e, carry):
            if first:
                for c in wcopy(e, True):
                    c.wait()
            grow = lax.rem(core * n_loc + e, n_exp)
            gcol = jnp.sum(jnp.where(lane8 == grow, g8, 0.0), axis=1, keepdims=True)
            x = x_view[...]
            g = jnp.dot(x, wg[e], preferred_element_type=F32)
            u = jnp.dot(x, wu[e], preferred_element_type=F32)
            act = (jax.nn.silu(g) * u).astype(BF)
            for hf in (0, 1):
                f = jnp.dot(act, wd[e, :, hf*half:(hf+1)*half], preferred_element_type=F32).astype(BF).astype(F32)
                acc[b, hf] = acc[b, hf] + gcol * f
            return carry
        acc[b] = jnp.zeros(acc.shape[1:], F32)
        lax.fori_loop(0, n_exp, step, 0)

    def rs(i, src, p):
        return remote(src, rbuf.at[i], rssem_s.at[i], rssem_r.at[i], p)
    for c in ag[3]:
        c.wait_recv()
    compute(3, True)
    c_xd = rs(0, acc.at[3, 0], peers[1]); c_xd.start()
    c_yd = rs(1, acc.at[3, 1], peers[2]); c_yd.start()
    for c in ag[1]:
        c.wait_recv()
    compute(1, False)
    c_xa = rs(2, acc.at[1, 0], peers[1]); c_xa.start()
    for c in ag[2]:
        c.wait_recv()
    compute(2, False)
    c_yb = rs(3, acc.at[2, 1], peers[2]); c_yb.start()
    c_yd.wait_recv()
    acc[1, 1] = acc[1, 1] + rbuf[1]
    c_xb = rs(4, acc.at[1, 1], peers[1]); c_xb.start()
    c_xd.wait_recv()
    acc[2, 0] = acc[2, 0] + rbuf[0]
    c_ya = rs(5, acc.at[2, 0], peers[2]); c_ya.start()
    compute(0, False)
    c_xa.wait_recv()
    c_ya.wait_recv()
    out_ref[:, :half] = (y_ref[:, :half] + ((acc[0, 0] + rbuf[2]) + rbuf[5])).astype(out_ref.dtype)
    c_yb.wait_recv()
    c_xb.wait_recv()
    out_ref[:, half:] = (y_ref[:, half:] + ((acc[0, 1] + rbuf[3]) + rbuf[4])).astype(out_ref.dtype)
    for b in (1, 2, 3):
        for c in ag[b]:
            c.wait_send()
    for c in (c_xd, c_yd, c_xa, c_yb, c_xb, c_ya):
        c.wait_send()

def moe_call(r, gt, y, w_gate, w_up, w_down, wg_p, wu_p, wd_p):
    n, d = r.shape
    nl, _, ff = w_gate.shape
    vm = pl.BlockSpec(memory_space=pltpu.VMEM)
    an = pl.BlockSpec(memory_space=pl.ANY)
    dma = pltpu.SemaphoreType.DMA
    return pl.pallas_call(moe_body,
        out_shape=jax.ShapeDtypeStruct((n, d), BF),
        in_specs=[vm, vm, vm] + [an]*6, out_specs=vm,
        scratch_shapes=[pltpu.VMEM((2*nl, d, ff), BF), pltpu.VMEM((2*nl, d, ff), BF), pltpu.VMEM((2*nl, ff, d), BF),
            pltpu.VMEM((3, n, d), BF), pltpu.VMEM((3, 2*nl, n), F32), pltpu.VMEM((4, 2, n, d//2), F32), pltpu.VMEM((6, n, d//2), F32),
            dma((3, 2*nl)), dma((2, 3)), dma((2, 3)), dma((6,)), dma((6,))],
        compiler_params=pltpu.CompilerParams(vmem_limit_bytes=60<<20, collective_id=1, has_side_effects=True), name="moe",
        cost_estimate=pl.CostEstimate(flops=26*10**9, bytes_accessed=30*10**6, transcendentals=0),
    )(r, gt, y, w_gate, w_up, w_down, wg_p, wu_p, wd_p)


def solution(mesh):
    n_group = mesh.shape['ep']
    row_spec = P(('dp', 'ep'), None)
    cache_spec = P(('dp', 'ep'), None, None, None)
    len_spec = P(('dp', 'ep'))
    rep_vec = P(None)
    rep_mat = P(None, None)
    exp_spec = P('ep', None, None)
    swap = [(i, i + 1 - 2 * (i % 2)) for i in range(n_group)]

    def local_step(hidden, k_cache, v_cache, seq_lens, expert_ids, ln_attn, w_q, w_k, w_v, q_gain, k_gain, w_o, ln_moe, w_router, w_gate, w_up, w_down):
        wg_p = lax.ppermute(w_gate, 'ep', swap)
        wu_p = lax.ppermute(w_up, 'ep', swap)
        wd_p = lax.ppermute(w_down, 'ep', swap)
        k_all, v_all, y_res, r_norm, gates = attn_call(hidden, k_cache, v_cache, seq_lens, expert_ids, ln_attn, w_q, w_k, w_v, q_gain, k_gain, w_o, ln_moe, w_router)
        out = moe_call(r_norm, gates, y_res, w_gate, w_up, w_down, wg_p, wu_p, wd_p)
        return out, k_all, v_all

    return jax.shard_map(local_step, mesh=mesh, in_specs=(row_spec, cache_spec, cache_spec, len_spec, row_spec, rep_vec, rep_mat, rep_mat, rep_mat, rep_vec, rep_vec, rep_mat, rep_vec, rep_mat, exp_spec, exp_spec, exp_spec), out_specs=(row_spec, cache_spec, cache_spec), check_vma=False)
```

time: 356 us -> 131 us (0.37)
  Pallas kernels: 0 us -> 123 us
  blocking collectives: 98.1 us -> 0 us
  matrix products: 72.4 us -> 0 us
  local copies, waits for them, and re-layouts: 65.5 us -> 3.95 us
  waiting for transfers between devices: 58.7 us -> 0.01 us
  other arithmetic: 56.3 us -> 1.29 us
    pallas_call x0 -> x2, Pallas kernels: none -> 123 us  [the longest x1 71.7 us: moe_call(): pl.pallas_call(moe_body, out_shape=jax.ShapeDtypeStruct((n, d), BF), in_s...]
    all_to_all x1 -> x0, blocking collectives: 98.1 us -> none  [local_step(): recv_rows = lax.all_to_all(send_rows, 'ep', 0, 0, tiled=True)]
    all_to_all x1 -> x0, waiting for transfers between devices: 58.7 us -> none  [local_step(): lax.all_to_all(out_rows.reshape(n_group * n_local, capacity, -1), 'ep', 0...]
    dot_general x9 -> x0, matrix products: 56.6 us -> none  [the longest x1 22.5 us: attend(): jnp.einsum('skgt,stkd->skgd', att_probs, v_all, preferred_element_type=jn...]
    gather x9 -> x0, local copies, waits for them, and re-layouts: 49.7 us -> none  [the longest x5 17.2 us: local_step(): jnp.take_along_axis(logits, expert_ids, axis=1)]
    select_n x2 -> x0, other arithmetic: 44 us -> none  [the longest x1 44 us: attend(): k_all = jnp.where(at_slot, k_new[:, None], k_cache)]
    sub x1 -> x0, matrix products: 15.8 us -> none  [attend(): att_probs = jax.nn.softmax(scores, axis=-1).astype(jnp.bfloat16)]
    convert_element_type x3 -> x1, local copies, waits for them, and re-layouts: 9.3 us -> 0.71 us  [attn_call(): gain = jnp.stack([q_gain, k_gain], axis=1).astype(F32)]
  transfers between devices with their start and end apart: 1 -> 3, of which waited for: 1 -> 0; matrix products, arithmetic and copies ran while one was open for 10% -> 3% of each run, Pallas kernels for 0% -> 40%
where the time goes in v1:
time: 131 us
  Pallas kernels  123 us (94%)
  local copies, waits for them, and re-layouts  3.95 us (3%)
  starting transfers between devices  1.39 us (1%)
    pallas_call x1, Pallas kernels, moe_call(): pl.pallas_call(moe_body, out_shape=jax.ShapeDtypeStruct((n, d), BF), in_s...  71.7 us
    pallas_call x1, Pallas kernels, attn_call(): pl.pallas_call(functools.partial(attn_body, cfg), out_shape=(jax.ShapeDty...  51.7 us
  transfers between devices with their start and end apart: 3, of which 0 were waited for; matrix products, arithmetic and copies ran while one was open for 3% of the time, Pallas kernels for 40%

profile of v1, /device:TPU:0, one launch (start us, length us, event | category | flops | bytes accessed | tf_op | source)
XLA Modules:
  0.0 130.7 jit_solution(15662208619671673484)
XLA Ops:
  0.6 0.9 collective-permute-start
  1.5 0.0 collective-permute-start.1
  1.5 0.5 collective-permute-start.2
  2.0 0.7 stack.18
  2.7 0.7 stack.19
  3.4 0.7 maximum_convert_fusion.1
  4.1 0.7 copy.24.gain_ref
  4.8 0.6 maximum_convert_fusion.vec_ref
  5.4 51.7 %attn.1 = (bf16[256,512,128]{2,1,0:T(8,128)(2,1)}, bf16[256,512,128]{2,1,0:T(8,128)(2,1)}, f32[256,1024]{1,0:T(8,128)}, bf16[256,1024]{1,0:T(8,128)(2,1)}, f32[32,256]{1,0:T(8,128)}) custom-call(s32[256]{0:T(256)} %lens_s.1, s32[1,256]{1,0:T(1,128)} %bitcast.23, s32[8,256]{1,0:T(8,128)} %bitcast.22, f32[2,1024]{1,0:T(2,128)} %maximum_convert_fusion.vec_ref, ...), custom_call_target="tpu_custom_call" | custom-call | flops 8000000000 | bytes 140000000 | tf_op jit(solution)/shard_map/attn/pallas_call | solution.py:148
  57.1 0.0 collective-permute-done.wg_par
  57.1 0.0 collective-permute-done.1.wu_par
  57.1 0.0 collective-permute-done.2.wd_par
  57.2 71.7 %moe.1 = bf16[256,1024]{1,0:T(8,128)(2,1)} custom-call(bf16[256,1024]{1,0:T(8,128)(2,1)} %get-tuple-element.8.r_ref, f32[32,256]{1,0:T(8,128)} %get-tuple-element.9.gt_ref, f32[256,1024]{1,0:T(8,128)} %get-tuple-element.10.y_ref, bf16[4,1024,512]{2,1,0:T(8,128)(2,1)} %wg_own.1, bf16[4,1024,512]{2,1,0:T(8,128)(2,1)} %wu_own.1, bf16[4,512,1024]{2,1,0:T(8,128)(2,1)} %wd_own.1, ...), custom_call_target="tpu_custom_call" | custom-call | flops 25999998976 | bytes 30000000 | tf_op jit(solution)/shard_map/moe/pallas_call | solution.py:270
  128.9 1.9 %copy.26 = bf16[256,1024]{1,0:T(8,128)(2,1)} copy(bf16[256,1024]{1,0:T(8,128)(2,1)} %moe.1) | data formatting | bytes 1048576
Async XLA Ops:
  0.6 56.5 %collective-permute-start = (bf16[4,1024,512]{2,1,0:T(8,128)(2,1)}, bf16[4,1024,512]{2,1,0:T(8,128)(2,1)}, u32[]{:S(2)}, u32[]{:S(2)}) collective-permute-start(bf16[4,1024,512]{2,1,0:T(8,128)(2,1)} %wg_own.1), channel_id=1, source_target_pairs={{0,1},{1,0},{2,3},{3,2},{4,5},{5,4},{6,7},{7,6}} | collective-permute-start | bytes 12582920 | tf_op jit(solution)/shard_map/ppermute | solution.py:292
  1.5 55.6 %collective-permute-start.1 = (bf16[4,1024,512]{2,1,0:T(8,128)(2,1)}, bf16[4,1024,512]{2,1,0:T(8,128)(2,1)}, u32[]{:S(2)}, u32[]{:S(2)}) collective-permute-start(bf16[4,1024,512]{2,1,0:T(8,128)(2,1)} %wu_own.1), channel_id=1, source_target_pairs={{0,1},{1,0},{2,3},{3,2},{4,5},{5,4},{6,7},{7,6}} | collective-permute-start | bytes 12582920 | tf_op jit(solution)/shard_map/ppermute | solution.py:293
  1.5 55.6 %collective-permute-start.2 = (bf16[4,512,1024]{2,1,0:T(8,128)(2,1)}, bf16[4,512,1024]{2,1,0:T(8,128)(2,1)}, u32[]{:S(2)}, u32[]{:S(2)}) collective-permute-start(bf16[4,512,1024]{2,1,0:T(8,128)(2,1)} %wd_own.1), channel_id=1, source_target_pairs={{0,1},{1,0},{2,3},{3,2},{4,5},{5,4},{6,7},{7,6}} | collective-permute-start | bytes 12582920 | tf_op jit(solution)/shard_map/ppermute | solution.py:294

commit v2 on v1

v2 whole, which is shorter than its diff:
```python
import functools
import numpy as np
import jax, jax.numpy as jnp
from jax import lax
from jax.experimental import pallas as pl
from jax.experimental.pallas import tpu as pltpu
from jax.sharding import PartitionSpec as P
EPS=1e-6; ROPE_BASE=1e6
F32=jnp.float32; BF=jnp.bfloat16

def attn_body(cfg, lens_s, lens_ref, ids_ref, vec_ref, gain_ref, freq_ref, h_hbm, wq_hbm, wk_hbm, wv_hbm, wo_hbm, wr_ref, k_hbm, v_hbm, *refs):
    sb, nb, lag, lo, later = cfg
    gp_ref = None
    if later:
        gp_ref = refs[2]
        refs = refs[3:]
    (ko_hbm, vo_hbm, y_ref, r_ref, gt_ref,
     kb, vb, wq, wk, wv, woe, woo, h_ref, qe_ref, qo_ref, kt_ref, vt_ref, ae_ref, ao_ref, isem, osem, wsem) = refs
    n = h_ref.shape[0]
    steps = n // sb
    per = 128 // sb
    n_kv, hd, dk = 8, 64, 512
    def cin(g, which):
        s = lax.rem(g, nb)
        r, b = ((k_hbm, kb), (v_hbm, vb))[which]
        return pltpu.make_async_copy(r.at[pl.ds(lo + g*sb, sb)], b.at[s], isem.at[which, s])
    def cout(g, which):
        s = lax.rem(g, nb)
        r, b = ((ko_hbm, kb), (vo_hbm, vb))[which]
        return pltpu.make_async_copy(b.at[s], r.at[pl.ds(lo + g*sb, sb)], osem.at[which, s])
    wcopies = [pltpu.make_async_copy(a, b, wsem.at[i]) for i, (a, b) in enumerate(
        ((h_hbm.at[pl.ds(lo, n)], h_ref), (wq_hbm, wq), (wk_hbm, wk), (wv_hbm, wv), (wo_hbm.at[:, 0], woe), (wo_hbm.at[:, 1], woo)))]
    for c in wcopies[:4]:
        c.start()
    for c in wcopies[:4]:
        c.wait()
    for g in range(nb):
        cin(g, 0).start(); cin(g, 1).start()
    for c in wcopies[4:]:
        c.start()
    h = h_ref[...].astype(F32)
    x = (h * lax.rsqrt(jnp.mean(h*h, axis=-1, keepdims=True) + EPS) * vec_ref[0:1, :]).astype(BF)
    ang = freq_ref[...] * lens_ref[:, lo:lo+n].astype(F32)
    cos_v = jnp.cos(ang)[None]; sin_v = jnp.sin(ang)[None]
    half = hd // 2
    def norm_rope(w_ref, gain):
        p = jnp.dot(x, w_ref[...], preferred_element_type=F32)
        p = p.T.reshape(-1, hd, n)
        p = p * lax.rsqrt(jnp.mean(p*p, axis=1, keepdims=True) + EPS) * gain[None]
        lo, hi = p[:, :half], p[:, half:]
        return jnp.concatenate([lo*cos_v - hi*sin_v, hi*cos_v + lo*sin_v], axis=1)
    q = norm_rope(wq, gain_ref[:, 0:1])
    q = q.reshape(n_kv, 2, hd, n)
    qe_ref[...] = q[:, 0].reshape(dk, n).T
    qo_ref[...] = q[:, 1].reshape(dk, n).T
    k = norm_rope(wk, gain_ref[:, 1:2]).reshape(dk, n).astype(BF).astype(F32)
    v = jnp.dot(x, wv[...], preferred_element_type=F32).T.astype(BF).astype(F32)
    for c in range(0, n, 128):
        w = min(128, n - c)
        kt_ref[c // 128, :, :w] = k[:, c:c+w]
        vt_ref[c // 128, :, :w] = v[:, c:c+w]

    lane = lax.broadcasted_iota(jnp.int32, (1, 128), 1)
    row = lax.broadcasted_iota(jnp.int32, (16, dk), 0)
    col = lax.broadcasted_iota(jnp.int32, (16, dk), 1) // hd
    m_even = row == col
    m_odd = row == col + n_kv

    zz = jnp.zeros((16, 128), BF)
    def fresh(t_ref, g, i):
        ln = lens_s[lo + g*sb + i]
        col = pltpu.roll(t_ref[g // per], lax.rem(ln - (lax.rem(g, per) * sb + i) + 128, 128), 1).astype(BF)
        return lane == ln, col
    def insert(buf, t_ref, g, p):
        slot = lax.rem(g, nb)
        for i in (2*p, 2*p+1):
            hit, col = fresh(t_ref, g, i)
            buf[slot, i] = jnp.where(hit, col, buf[slot, i])
    def scores(g, p, qe, qo):
        slot = lax.rem(g, nb)
        qs = [jnp.where(m_even, qe[i:i+1], jnp.where(m_odd, qo[i:i+1], 0.0)).astype(BF) for i in (2*p, 2*p+1)]
        ks = jnp.concatenate([kb[slot, 2*p], kb[slot, 2*p+1]], axis=1)
        s = jnp.dot(jnp.concatenate(qs, axis=0), ks, preferred_element_type=F32)
        return [jnp.where(lane <= lens_s[lo + g*sb + 2*p + j], s[16*j:16*j+16, 128*j:128*j+128] * (hd ** -0.5), -1e30) for j in (0, 1)]
    def combine(g, p, pr):
        slot = lax.rem(g, nb)
        p0 = pr[32*p:32*p+16]; p1 = pr[32*p+16:32*p+32]
        pp = jnp.concatenate([jnp.concatenate([p0, zz], axis=1), jnp.concatenate([zz, p1], axis=1)], axis=0)
        vv = jnp.concatenate([vb[slot, 2*p], vb[slot, 2*p+1]], axis=1)
        o = lax.dot_general(pp, vv, (((1,), (1,)), ((), ())), preferred_element_type=F32)
        ev = []; od = []
        for j in (0, 1):
            oj = o[16*j:16*j+16]
            ev.append(jnp.sum(jnp.where(m_even[:8], oj[:8], 0.0), axis=0, keepdims=True))
            od.append(jnp.sum(jnp.where(m_even[:8], oj[8:], 0.0), axis=0, keepdims=True))
        return ev, od
    def attend(g, nxt):
        rows = pl.ds(pl.multiple_of(g*sb, sb), sb)
        qe = qe_ref[rows, :]
        qo = qo_ref[rows, :]
        sc = []
        for p in range(sb // 2):
            sc += scores(g, p, qe, qo)
            if nxt is not None:
                insert(kb, kt_ref, nxt, p)
        s = jnp.concatenate(sc, axis=0)
        e = jnp.exp(s - jnp.max(s, axis=-1, keepdims=True))
        pr = (e / jnp.sum(e, axis=-1, keepdims=True)).astype(BF)
        oe = []; oo = []
        for p in range(sb // 2):
            ev, od = combine(g, p, pr)
            oe += ev; oo += od
            if nxt is not None:
                insert(vb, vt_ref, nxt, p)
        ae_ref[rows, :] = jnp.concatenate(oe, axis=0)
        ao_ref[rows, :] = jnp.concatenate(oo, axis=0)

    cin(0, 0).wait(); cin(0, 1).wait()
    for p in range(sb // 2):
        insert(kb, kt_ref, jnp.int32(0), p)
        insert(vb, vt_ref, jnp.int32(0), p)
    cout(0, 0).start(); cout(0, 1).start()

    @pl.loop(0, steps - 1)
    def _(g):
        @pl.when((g >= lag) & (g - lag + nb < steps))
        def _():
            cout(g - lag, 0).wait(); cout(g - lag, 1).wait()
            cin(g - lag + nb, 0).start(); cin(g - lag + nb, 1).start()
        cin(g + 1, 0).wait(); cin(g + 1, 1).wait()
        attend(g, g + 1)
        cout(g + 1, 0).start(); cout(g + 1, 1).start()
    attend(jnp.int32(steps - 1), None)

    for c in wcopies[4:]:
        c.wait()
    y = h_ref[...].astype(F32)
    y = y + (jnp.dot(ae_ref[...].astype(BF), woe[...].reshape(dk, -1), preferred_element_type=F32)
             + jnp.dot(ao_ref[...].astype(BF), woo[...].reshape(dk, -1), preferred_element_type=F32))
    y_ref[...] = y
    r = (y * lax.rsqrt(jnp.mean(y*y, axis=-1, keepdims=True) + EPS) * vec_ref[1:2, :]).astype(BF)
    r_ref[...] = r
    lg = lax.dot_general(wr_ref[...], r, (((1,), (1,)), ((), ())), preferred_element_type=F32)
    eid = lax.broadcasted_iota(jnp.int32, lg.shape, 0)
    ids = ids_ref[:, lo:lo+n]
    hot = eid == ids[0:1]
    for j in range(1, ids.shape[0]):
        hot = hot | (eid == ids[j:j+1])
    lg = jnp.where(hot, lg, -jnp.inf)
    e = jnp.where(hot, jnp.exp(lg - jnp.max(lg, axis=0, keepdims=True)), 0.0)
    if later:
        gt_ref[:, :lo] = gp_ref[...]
    gt_ref[:, lo:] = e / jnp.sum(e, axis=0, keepdims=True)
    for j in range(nb):
        cout(steps - nb + j, 0).wait(); cout(steps - nb + j, 1).wait()

def attn_call(arrays, consts, lo, n, prev=None, cfg=(8, 8, 3)):
    hidden, kc, vc, seq_lens, lens_row, ids_t, w_q, w_k, w_v, w_o4, w_rt = arrays
    vec, gain, freq = consts
    d = hidden.shape[1]
    _, dk, t = kc.shape
    nk, _, hd, _ = w_o4.shape
    sb, nb, lag = cfg
    ne = w_rt.shape[0]
    nc = -(-n // 128)
    vm = pl.BlockSpec(memory_space=pltpu.VMEM)
    an = pl.BlockSpec(memory_space=pl.ANY)
    sm = pl.BlockSpec(memory_space=pltpu.SMEM)
    args = [seq_lens, lens_row, ids_t, vec, gain, freq, hidden, w_q, w_k, w_v, w_o4, w_rt, kc, vc]
    specs = [sm, vm, vm, vm, vm, vm, an, an, an, an, an, vm, an, an]
    alias = {}
    if prev is not None:
        args += list(prev)
        specs += [an, an, vm]
        alias = {14: 0, 15: 1}
    frac = n / hidden.shape[0]
    return pl.pallas_call(functools.partial(attn_body, cfg + (lo, prev is not None)),
        out_shape=(jax.ShapeDtypeStruct(kc.shape, BF), jax.ShapeDtypeStruct(vc.shape, BF), jax.ShapeDtypeStruct((n, d), F32),
                   jax.ShapeDtypeStruct((n, d), BF), jax.ShapeDtypeStruct((ne, lo + n), F32)),
        in_specs=specs, out_specs=(an, an, vm, vm, vm), input_output_aliases=alias,
        scratch_shapes=[pltpu.VMEM((nb, sb, dk, t), BF), pltpu.VMEM((nb, sb, dk, t), BF),
            pltpu.VMEM(w_q.shape, BF), pltpu.VMEM(w_k.shape, BF), pltpu.VMEM(w_v.shape, BF),
            pltpu.VMEM((nk, hd, d), BF), pltpu.VMEM((nk, hd, d), BF), pltpu.VMEM((n, d), BF),
            pltpu.VMEM((n, dk), F32), pltpu.VMEM((n, dk), F32), pltpu.VMEM((nc, dk, 128), F32), pltpu.VMEM((nc, dk, 128), F32),
            pltpu.VMEM((n, dk), F32), pltpu.VMEM((n, dk), F32),
            pltpu.SemaphoreType.DMA((2, nb)), pltpu.SemaphoreType.DMA((2, nb)), pltpu.SemaphoreType.DMA((6,))],
        compiler_params=pltpu.CompilerParams(vmem_limit_bytes=60<<20), name="attn",
        cost_estimate=pl.CostEstimate(flops=int(40*10**9*frac), bytes_accessed=int(140*10**6*frac), transcendentals=0),
    )(*args)

def attn_inputs(hidden, k_cache, v_cache, seq_lens, expert_ids, ln_attn, w_q, w_k, w_v, q_gain, k_gain, w_o, ln_moe, w_router):
    n, d = hidden.shape
    t = k_cache.shape[1]; dk = w_k.shape[1]; hd = q_gain.shape[0]; nk = dk // hd
    kc = k_cache.transpose(0, 2, 3, 1).reshape(n, dk, t)
    vc = v_cache.transpose(0, 2, 3, 1).reshape(n, dk, t)
    vec = jnp.stack([ln_attn, ln_moe]).astype(F32)
    gain = jnp.stack([q_gain, k_gain], axis=1).astype(F32)
    freq = jnp.asarray(np.power(np.float32(ROPE_BASE), -np.arange(0, hd, 2).astype(np.float32) / np.float32(hd)).astype(np.float32).reshape(-1, 1))
    arrays = (hidden, kc, vc, seq_lens, seq_lens.reshape(1, n), expert_ids.T, w_q, w_k, w_v, w_o.reshape(nk, 2, hd, d), w_router.T)
    back = lambda z: z.reshape(n, nk, hd, t).transpose(0, 3, 1, 2)
    return arrays, (vec, gain, freq), back


def moe_body(r_ref, gt_ref, y_hbm, wg_own, wu_own, wd_own, wg_par, wu_par, wd_par, out_ref,
             wg, wu, wd, xr, gts, y_ref, act, acc, rbuf, wsem, ysem, agsem_s, agsem_r, gsem_s, gsem_r, rssem_s, rssem_r):
    me = lax.axis_index('ep')
    core = me % 2
    xpos = (me // 2) % 2
    ypos = me // 4
    OWN, X, Y, D = 0, 1, 2, 3
    peers = [None, ypos*4 + (1-xpos)*2 + core, (1-ypos)*4 + xpos*2 + core, (1-ypos)*4 + (1-xpos)*2 + core]
    n_loc = wg_own.shape[0]
    n_exp = 2*n_loc
    hr, hc = acc.shape[3], acc.shape[4]
    ff = wg.shape[2]

    barrier = pltpu.get_barrier_semaphore()
    for p in peers[1:]:
        pl.semaphore_signal(barrier, inc=1, device_id={"ep": p}, device_id_type=pl.DeviceIdType.MESH)

    def wcopy(e, own):
        src = (wg_own, wu_own, wd_own) if own else (wg_par, wu_par, wd_par)
        s = lax.rem(e, n_loc)
        return [pltpu.make_async_copy(a.at[s], b.at[e], wsem.at[i, e]) for i, (a, b) in enumerate(zip(src, (wg, wu, wd)))]
    for e in range(n_exp):
        for c in wcopy(jnp.int32(e), e < n_loc):
            c.start()
    ycopy = pltpu.make_async_copy(y_hbm, y_ref, ysem.at[0])
    ycopy.start()
    pl.semaphore_wait(barrier, 3)

    def remote(src, dst, ss, rs, p):
        return pltpu.make_async_remote_copy(src_ref=src, dst_ref=dst, send_sem=ss, recv_sem=rs,
                                            device_id={"ep": p}, device_id_type=pl.DeviceIdType.MESH)
    ag = {}
    gc = {}
    for b in (D, X, Y):
        rows8 = pl.ds(pl.multiple_of((peers[b] // 2) * n_exp, n_exp), n_exp)
        gc[b] = remote(gt_ref.at[rows8], gts.at[b-1], gsem_s.at[b-1], gsem_r.at[b-1], peers[b])
        gc[b].start()
    for b, h in ((D, 0), (D, 1), (X, 0), (Y, 0), (X, 1), (Y, 1)):
        rows = pl.ds(h*hr, hr)
        ag[b, h] = remote(r_ref.at[rows], xr.at[b-1, rows], agsem_s.at[b-1, h], agsem_r.at[b-1, h], peers[b])
        ag[b, h].start()

    def gates(b):
        if b == OWN:
            return gt_ref[pl.ds(pl.multiple_of((me // 2) * n_exp, n_exp), n_exp), :].T
        return gts[b-1].T

    def compute(load, g8, bs, hs, first=False):
        m = len(bs) * len(hs) * hr
        b0, nb, h0, nh = bs[0], len(bs), hs[0], len(hs)
        lane8 = lax.broadcasted_iota(jnp.int32, (m, n_exp), 1)
        for b in bs:
            for h in hs:
                acc[b, h] = jnp.zeros(acc.shape[2:], F32)
        def step(e, carry):
            if first:
                for c in wcopy(e, True):
                    c.wait()
            gcol = jnp.sum(jnp.where(lane8 == lax.rem(core * n_loc + e, n_exp), g8, 0.0), axis=1, keepdims=True)
            x = load()
            for q in range(2):
                cols = slice(q*ff//2, (q+1)*ff//2)
                g = jnp.dot(x, wg[e, :, cols], preferred_element_type=F32)
                u = jnp.dot(x, wu[e, :, cols], preferred_element_type=F32)
                act[:m, cols] = (jax.nn.silu(g) * u).astype(BF)
            a = act[:m]
            for q in range(4):
                w = hc // 2
                s = (q % 2) * w
                f = jnp.dot(a, wd[e, :, q*w:(q+1)*w], preferred_element_type=F32).astype(BF).astype(F32) * gcol
                i = 0
                for b in bs:
                    for h in hs:
                        acc[b, h, q//2, :, s:s+w] = acc[b, h, q//2, :, s:s+w] + f[i*hr:(i+1)*hr]
                        i += 1
            return carry
        lax.fori_loop(0, n_exp, step, 0)

    def rs(i, h, src, p):
        return remote(src, rbuf.at[i, h], rssem_s.at[i, h], rssem_r.at[i, h], p)
    sent = {}
    def send(i, h, src, b):
        sent[i, h] = rs(i, h, src, peers[b])
        sent[i, h].start()

    compute(lambda: r_ref[...], gates(OWN), (OWN,), (0, 1), first=True)
    gc[D].wait_recv()
    ag[D, 0].wait_recv(); ag[D, 1].wait_recv()
    compute(lambda: xr[D-1], gates(D), (D,), (0, 1))
    for h in (0, 1):
        send(0, h, acc.at[D, h, 0], X)
        send(1, h, acc.at[D, h, 1], Y)
    gc[X].wait_recv()
    gc[Y].wait_recv()
    gx, gy = gates(X), gates(Y)
    for h in (0, 1):
        rows = slice(h*hr, (h+1)*hr)
        ag[X, h].wait_recv(); ag[Y, h].wait_recv()
        compute(lambda: jnp.concatenate([xr[X-1, rows], xr[Y-1, rows]], axis=0), jnp.concatenate([gx[rows], gy[rows]], axis=0), (X, Y), (h,))
        send(2, h, acc.at[X, h, 0], X)
        send(3, h, acc.at[Y, h, 1], Y)
        sent[1, h].wait_recv()
        acc[X, h, 1] = acc[X, h, 1] + rbuf[1, h]
        send(4, h, acc.at[X, h, 1], X)
        sent[0, h].wait_recv()
        acc[Y, h, 0] = acc[Y, h, 0] + rbuf[0, h]
        send(5, h, acc.at[Y, h, 0], Y)
    ycopy.wait()
    for h in (0, 1):
        rows = slice(h*hr, (h+1)*hr)
        sent[2, h].wait_recv()
        sent[3, h].wait_recv()
        acc[OWN, h, 0] = y_ref[rows, :hc] + (acc[OWN, h, 0] + rbuf[2, h])
        acc[OWN, h, 1] = y_ref[rows, hc:] + (acc[OWN, h, 1] + rbuf[3, h])
        sent[5, h].wait_recv()
        out_ref[rows, :hc] = (acc[OWN, h, 0] + rbuf[5, h]).astype(out_ref.dtype)
        sent[4, h].wait_recv()
        out_ref[rows, hc:] = (acc[OWN, h, 1] + rbuf[4, h]).astype(out_ref.dtype)
    for c in (*gc.values(), *ag.values(), *sent.values()):
        c.wait_send()

def moe_call(r, gt, y, w_gate, w_up, w_down, wg_p, wu_p, wd_p):
    n, d = r.shape
    nl, _, ff = w_gate.shape
    vm = pl.BlockSpec(memory_space=pltpu.VMEM)
    an = pl.BlockSpec(memory_space=pl.ANY)
    dma = pltpu.SemaphoreType.DMA
    return pl.pallas_call(moe_body,
        out_shape=jax.ShapeDtypeStruct((n, d), BF),
        in_specs=[vm, vm] + [an]*7, out_specs=vm,
        scratch_shapes=[pltpu.VMEM((2*nl, d, ff), BF), pltpu.VMEM((2*nl, d, ff), BF), pltpu.VMEM((2*nl, ff, d), BF),
            pltpu.VMEM((3, n, d), BF), pltpu.VMEM((3, 2*nl, n), F32), pltpu.VMEM((n, d), F32), pltpu.VMEM((n, ff), BF),
            pltpu.VMEM((4, 2, 2, n//2, d//2), F32), pltpu.VMEM((6, 2, n//2, d//2), F32),
            dma((3, 2*nl)), dma((1,)), dma((3, 2)), dma((3, 2)), dma((3,)), dma((3,)), dma((6, 2)), dma((6, 2))],
        compiler_params=pltpu.CompilerParams(vmem_limit_bytes=60<<20, collective_id=1, has_side_effects=True), name="moe",
        cost_estimate=pl.CostEstimate(flops=26*10**9, bytes_accessed=30*10**6, transcendentals=0),
    )(r, gt, y, w_gate, w_up, w_down, wg_p, wu_p, wd_p)


def solution(mesh):
    n_group = mesh.shape['ep']
    row_spec = P(('dp', 'ep'), None)
    cache_spec = P(('dp', 'ep'), None, None, None)
    len_spec = P(('dp', 'ep'))
    rep_vec = P(None)
    rep_mat = P(None, None)
    exp_spec = P('ep', None, None)
    swap = [(i, i + 1 - 2 * (i % 2)) for i in range(n_group)]

    def local_step(hidden, k_cache, v_cache, seq_lens, expert_ids, ln_attn, w_q, w_k, w_v, q_gain, k_gain, w_o, ln_moe, w_router, w_gate, w_up, w_down):
        wg_p = lax.ppermute(w_gate, 'ep', swap)
        wu_p = lax.ppermute(w_up, 'ep', swap)
        wd_p = lax.ppermute(w_down, 'ep', swap)
        arrays, consts, back = attn_inputs(hidden, k_cache, v_cache, seq_lens, expert_ids, ln_attn, w_q, w_k, w_v, q_gain, k_gain, w_o, ln_moe, w_router)
        ko, vo, y, r, gt = attn_call(arrays, consts, 0, hidden.shape[0])
        out = moe_call(r, gt, y, w_gate, w_up, w_down, wg_p, wu_p, wd_p)
        return out, back(ko), back(vo)

    return jax.shard_map(local_step, mesh=mesh, in_specs=(row_spec, cache_spec, cache_spec, len_spec, row_spec, rep_vec, rep_mat, rep_mat, rep_mat, rep_vec, rep_vec, rep_mat, rep_vec, rep_mat, exp_spec, exp_spec, exp_spec), out_specs=(row_spec, cache_spec, cache_spec), check_vma=False)
```

time: 131 us -> 123 us (0.939)
  Pallas kernels: 123 us -> 115 us
    pallas_call x1, Pallas kernels: 71.7 us -> 64.2 us  [moe_call(): pl.pallas_call(moe_body, out_shape=jax.ShapeDtypeStruct((n, d), BF), in_s...]
  transfers between devices with their start and end apart: 3 -> 3, of which waited for: 0 -> 0; matrix products, arithmetic and copies ran while one was open for 3% -> 3% of each run, Pallas kernels for 40% -> 42%
where the time goes in v2:
time: 123 us
  Pallas kernels  115 us (93%)
  local copies, waits for them, and re-layouts  3.95 us (3%)
  starting transfers between devices  1.39 us (1%)
  other arithmetic  1.29 us (1%)
    pallas_call x1, Pallas kernels, moe_call(): pl.pallas_call(moe_body, out_shape=jax.ShapeDtypeStruct((n, d), BF), in_s...  64.2 us
    pallas_call x1, Pallas kernels, attn_call(): pl.pallas_call(functools.partial(attn_body, cfg + (lo, prev is not None))...  51.2 us
  transfers between devices with their start and end apart: 3, of which 0 were waited for; matrix products, arithmetic and copies ran while one was open for 3% of the time, Pallas kernels for 42%

profile of v2, /device:TPU:0, one launch (start us, length us, event | category | flops | bytes accessed | tf_op | source)
XLA Modules:
  0.0 122.7 jit_solution(10415386050747545288)
XLA Ops:
  0.6 0.9 collective-permute-start
  1.5 0.0 collective-permute-start.1
  1.5 0.5 collective-permute-start.2
  2.0 0.7 stack.18
  2.7 0.7 stack.19
  3.4 0.7 maximum_convert_fusion.1
  4.1 0.7 copy.24.gain_ref
  4.8 0.6 maximum_convert_fusion.vec_ref
  5.4 51.2 %attn.1 = (bf16[256,512,128]{2,1,0:T(8,128)(2,1)}, bf16[256,512,128]{2,1,0:T(8,128)(2,1)}, f32[256,1024]{1,0:T(8,128)}, bf16[256,1024]{1,0:T(8,128)(2,1)}, f32[32,256]{1,0:T(8,128)}) custom-call(s32[256]{0:T(256)} %lens_s.1, s32[1,256]{1,0:T(1,128)} %bitcast.25, s32[8,256]{1,0:T(8,128)} %bitcast.24, f32[2,1024]{1,0:T(2,128)} %maximum_convert_fusion.vec_ref, ...), custom_call_target="tpu_custom_call" | custom-call | flops 40000000000 | bytes 140000000 | tf_op jit(solution)/shard_map/attn/pallas_call | solution.py:177
  56.6 0.0 collective-permute-done.wg_par
  56.6 0.0 collective-permute-done.1.wu_par
  56.6 0.0 collective-permute-done.2.wd_par
  56.6 64.2 %moe.1 = bf16[256,1024]{1,0:T(8,128)(2,1)} custom-call(bf16[256,1024]{1,0:T(8,128)(2,1)} %get-tuple-element.8.r_ref, f32[32,256]{1,0:T(8,128)} %get-tuple-element.9.gt_ref, f32[256,1024]{1,0:T(8,128)} %get-tuple-element.10.y_hbm, bf16[4,1024,512]{2,1,0:T(8,128)(2,1)} %wg_own.1, bf16[4,1024,512]{2,1,0:T(8,128)(2,1)} %wu_own.1, bf16[4,512,1024]{2,1,0:T(8,128)(2,1)} %wd_own.1, ...), custom_call_target="tpu_custom_call" | custom-call | flops 25999998976 | bytes 30000000 | tf_op jit(solution)/shard_map/moe/pallas_call | solution.py:331
  120.8 1.9 %copy.26 = bf16[256,1024]{1,0:T(8,128)(2,1)} copy(bf16[256,1024]{1,0:T(8,128)(2,1)} %moe.1) | data formatting | bytes 1048576
Async XLA Ops:
  0.6 56.0 %collective-permute-start = (bf16[4,1024,512]{2,1,0:T(8,128)(2,1)}, bf16[4,1024,512]{2,1,0:T(8,128)(2,1)}, u32[]{:S(2)}, u32[]{:S(2)}) collective-permute-start(bf16[4,1024,512]{2,1,0:T(8,128)(2,1)} %wg_own.1), channel_id=1, source_target_pairs={{0,1},{1,0},{2,3},{3,2},{4,5},{5,4},{6,7},{7,6}} | collective-permute-start | bytes 12582920 | tf_op jit(solution)/shard_map/ppermute | solution.py:354
  1.5 55.1 %collective-permute-start.1 = (bf16[4,1024,512]{2,1,0:T(8,128)(2,1)}, bf16[4,1024,512]{2,1,0:T(8,128)(2,1)}, u32[]{:S(2)}, u32[]{:S(2)}) collective-permute-start(bf16[4,1024,512]{2,1,0:T(8,128)(2,1)} %wu_own.1), channel_id=1, source_target_pairs={{0,1},{1,0},{2,3},{3,2},{4,5},{5,4},{6,7},{7,6}} | collective-permute-start | bytes 12582920 | tf_op jit(solution)/shard_map/ppermute | solution.py:355
  1.5 55.1 %collective-permute-start.2 = (bf16[4,512,1024]{2,1,0:T(8,128)(2,1)}, bf16[4,512,1024]{2,1,0:T(8,128)(2,1)}, u32[]{:S(2)}, u32[]{:S(2)}) collective-permute-start(bf16[4,512,1024]{2,1,0:T(8,128)(2,1)} %wd_own.1), channel_id=1, source_target_pairs={{0,1},{1,0},{2,3},{3,2},{4,5},{5,4},{6,7},{7,6}} | collective-permute-start | bytes 12582920 | tf_op jit(solution)/shard_map/ppermute | solution.py:356
